TPU v7x, 128 devices: a whole 4x4x4 slice. The times are simulated.
128 devices in a mesh: ep: 32 (over y, z, core), dp: 4 (over x).
Axes of the slice: x: 4, y: 4, z: 4, core: 2. Of those that a mesh axis runs over, the one named last changes fastest.
Arguments:
- lengths: int32 [128, 16], P(('ep', 'dp')), may hold values from 1 to 512, as said below
- id_lists: int32 [128, 16, 512], P(('ep', 'dp')), may hold values from 0 to 65535, as said below
- feature_slots: int32 [16], replicated, may hold values from 0 to 15, each once
- embedding_table: bfloat16 [1048576, 128], P(('ep', 'dp')), may hold values from -6 to 6
Outputs:
- embedded: bfloat16 [128, 16, 512, 128], P(('ep', 'dp'))
Inputs may be any that keep to these rules, and one draw needn't show every extreme that they name: `lengths`: every user has some feature whose length is exactly 512. `id_lists`: among the valid entries (positions below the list's length) of the 1 users of one device, at most 80 ids lie in any one block of 512 ids that starts at a multiple of 512; in every draw some block holds exactly 80 valid ids from every device. Entries past a list's length hold arbitrary ids of the range.
All inputs are finite; a program needn't handle non-finite values.
Results may differ from a plain program's by a relative error of at most 0.001.
Values may be sent and summed in bfloat16 or wider, within the bound.
No kernel may reach another device: no remote copies, remote signals or barrier semaphores. Data moves between devices by JAX's collectives and lax.ppermute only.
A program may use at most 64 MiB of HBM per device.

v0:
```python
import jax
import jax.numpy as jnp
from jax import lax
from jax.sharding import PartitionSpec as P


def on_device(lengths, id_lists, feature_slots, embedding_table):
    num_users, num_feats, list_span = id_lists.shape
    row_width = embedding_table.shape[1]
    ep_count = lax.axis_size("ep")
    dp_count = lax.axis_size("dp")
    owners = ep_count * dp_count
    per_owner = embedding_table.shape[0] // num_feats
    slot_total = num_users * num_feats * list_span
    capacity = 5 * slot_total // (4 * owners)
    dump_slot = owners * capacity
    block_rows = 512
    block_count = slot_total // block_rows
    position = lax.broadcasted_iota(jnp.int32, id_lists.shape, 2)
    live_mask = (position < lengths[:, :, None]).reshape(block_count, block_rows)
    flat_ids = id_lists.reshape(slot_total)
    owner_of = flat_ids // per_owner
    feature_of = jnp.broadcast_to(feature_slots[None, :, None], id_lists.shape).reshape(slot_total)
    local_row = (flat_ids - owner_of * per_owner) * num_feats + feature_of
    owner_of = owner_of.reshape(block_count, block_rows)
    local_row = local_row.reshape(block_count, block_rows)
    owner_column = jnp.arange(owners, dtype=jnp.int32)
    rank_column = jnp.arange(capacity, dtype=jnp.int32)
    row_iota = lax.broadcasted_iota(jnp.int32, (block_rows, block_rows), 0)
    col_iota = lax.broadcasted_iota(jnp.int32, (block_rows, block_rows), 1)
    earlier = (row_iota > col_iota).astype(jnp.bfloat16)

    def rank_block(carry, inputs):
        offset, request = carry
        owner_block, live_block, row_block = inputs
        hot = (owner_block[:, None] == owner_column[None, :]) & live_block[:, None]
        hot_flt = hot.astype(jnp.float32)
        within = jnp.dot(earlier, hot.astype(jnp.bfloat16), preferred_element_type=jnp.float32)
        before = within + offset[None, :]
        rank_int = jnp.sum(before * hot_flt, axis=1).astype(jnp.int32)
        rank_hot = (rank_int[:, None] == rank_column[None, :]).astype(jnp.float32)
        weighted = hot_flt * row_block.astype(jnp.float32)[:, None]
        added = lax.dot_general(
            weighted,
            rank_hot,
            (((0,), (0,)), ((), ())),
            precision=lax.Precision.HIGHEST,
            preferred_element_type=jnp.float32,
        )
        offset = offset + jnp.sum(hot_flt, axis=0)
        target_block = jnp.where(live_block, owner_block * capacity + rank_int, dump_slot)
        return ((offset, request + added), target_block)

    start = (jnp.zeros((owners,), jnp.float32), jnp.zeros((owners, capacity), jnp.float32))
    (unused_offset, request_flt), targets = lax.scan(
        rank_block, start, (owner_of, live_mask, local_row)
    )
    request = request_flt.astype(jnp.int32)
    incoming = lax.all_to_all(request, ("ep", "dp"), split_axis=0, concat_axis=0, tiled=True)
    replies = jnp.take(embedding_table, incoming, axis=0)
    returned = lax.all_to_all(
        replies, ("ep", "dp"), split_axis=0, concat_axis=0, tiled=True
    ).reshape(owners * capacity, row_width)
    slot_column = jnp.arange(dump_slot, dtype=jnp.int32)

    def place_block(target_block):
        select = (target_block[:, None] == slot_column[None, :]).astype(jnp.bfloat16)
        return jnp.dot(select, returned, preferred_element_type=jnp.float32).astype(jnp.bfloat16)

    embedded = lax.map(place_block, targets)
    return embedded.reshape(num_users, num_feats, list_span, row_width)


def solution(mesh):
    placed = (P(("ep", "dp"), None), P(("ep", "dp"), None, None), P(), P(("ep", "dp"), None))
    return jax.shard_map(
        on_device,
        mesh=mesh,
        in_specs=placed,
        out_specs=P(("ep", "dp"), None, None, None),
        check_vma=False,
    )
```

profile of v0, /device:TPU:1, one launch (start us, length us, event | category | flops | bytes accessed | tf_op | source)
XLA Modules:
  0.0 220.5 jit_solution(4914755391864331398)
XLA Ops:
  0.0 0.9 iota_compare_fusion.12
  0.9 0.8 fusion.33
  1.7 18.6 %while.29 = (s32[]{:T(128)}, f32[128]{0:T(128)S(1)}, f32[128,80]{0,1:T(8,128)S(1)}, s32[16,512]{1,0:T(8,128)S(1)}, s32[16,512]{1,0:T(8,128)S(1)}, /*index=5*/pred[16,512]{1,0:T(8,128)(4,1)S(1)}, s32[16,512]{1,0:T(8,128)S(1)}) while((s32[]{:T(128)}, f32[128]{0:T(128)S(1)}, f32[128,80]{0,1:T(8,128)S(1)}, ...), condition=%wide.region_3.4_spmd.clone.clone, body=%wide.region_0.3_spmd.clone.sunk.clone | while | flops 131528832 | bytes 122984 | solution.py:55
  1.9 0.3 fusion.57
  2.3 0.5 convolution_add_fusion.4
  3.1 0.3 fusion.57
  3.4 0.5 convolution_add_fusion.4
  4.2 0.3 fusion.57
  4.6 0.5 convolution_add_fusion.4
  5.4 0.3 fusion.57
  5.7 0.5 convolution_add_fusion.4
  6.6 0.3 fusion.57
  6.9 0.5 convolution_add_fusion.4
  8.1 0.5 convolution_add_fusion.4
  9.2 0.5 convolution_add_fusion.4
  10.0 0.3 fusion.57
  10.4 0.5 convolution_add_fusion.4
  11.6 0.5 convolution_add_fusion.4
  12.7 0.5 convolution_add_fusion.4
  13.9 0.5 convolution_add_fusion.4
  15.0 0.5 convolution_add_fusion.4
  16.2 0.5 convolution_add_fusion.4
  17.4 0.5 convolution_add_fusion.4
  18.2 0.3 fusion.57
  18.5 0.5 convolution_add_fusion.4
  19.7 0.5 convolution_add_fusion.4
  20.4 21.2 %all_to_all.20 = s32[128,1,80]{2,1,0:T(1,128)S(1)} all-to-all(s32[128,1,80]{2,1,0:T(1,128)S(1)} %bitcast.71), channel_id=1, replica_groups=mesh['ep'=32,'dp'=4] {'ep','dp'}, dimensions={0} | all-to-all | bytes 81920 | tf_op jit(solution)/shard_map/all_to_all | solution.py:59
  41.8 36.2 %gather_fusion = bf16[10240,128]{1,0:T(8,128)(2,1)} fusion(bf16[8192,128]{1,0:T(8,128)(2,1)S(1)} %copy-done, s32[10240]{0:T(1024)S(1)} %broadcast_clamp_fusion), kind=kCustom, calls=%fused_computation | custom fusion | bytes 5283840 | tf_op jit(solution)/shard_map/jit(_take)/gather | solution.py:60
  78.0 6.5 %broadcast_select_fusion.1 = bf16[128,80,128]{2,1,0:T(8,128)(2,1)} fusion(bf16[128,80,128]{2,1,0:T(8,128)(2,1)} %bitcast.68, pred[128,80]{1,0:T(8,128)(4,1)S(1)} %compare_and_fusion), kind=kLoop, calls=%fused_computation.37 | loop fusion | flops 1310720 | bytes 5253120 | tf_op jit(solution)/shard_map/jit(_take)/select_n | solution.py:60
  84.4 4.8 %all-to-all-start.1 = ((bf16[128,80,128]{2,1,0:T(8,128)(2,1)}), bf16[128,80,128]{2,1,0:T(8,128)(2,1)}, u32[]{:S(2)}, u32[]{:S(2)}) async-start(bf16[128,80,128]{2,1,0:T(8,128)(2,1)} %broadcast_select_fusion.1), calls=%async_computation.1 | async-start | bytes 5242880 | tf_op jit(solution)/shard_map/all_to_all | solution.py:61
  89.3 36.4 %all-to-all-done.1 = bf16[128,80,128]{2,1,0:T(8,128)(2,1)} async-done(((bf16[128,80,128]{2,1,0:T(8,128)(2,1)}), bf16[128,80,128]{2,1,0:T(8,128)(2,1)}, u32[]{:S(2)}, u32[]{:S(2)}) %all-to-all-start.1) | async-done | bytes 2621472 | tf_op jit(solution)/shard_map/all_to_all | solution.py:61
  125.7 94.8 %while.28 = (s32[]{:T(128)}, bf16[16,512,128]{2,1,0:T(8,128)(2,1)}, s32[16,512]{1,0:T(8,128)S(1)}, bf16[10240,128]{1,0:T(8,128)(2,1)}) while((s32[]{:T(128)}, bf16[16,512,128]{2,1,0:T(8,128)(2,1)}, s32[16,512]{1,0:T(8,128)S(1)}, bf16[10240,128]{1,0:T(8,128)(2,1)}) %tuple.56), condition=%wide.region_5.6_spmd.clone.clone, body=%wide.region_4.5_spmd.clone.sunk.clone | while | flops 1347485696 | bytes 2759225 | solution.py:70
  125.7 5.9 %fusion.52 = bf16[16,512,128]{2,1,0:T(8,128)(2,1)} fusion(bf16[16,512,128]{2,1,0:T(8,128)(2,1)} %get-tuple-element.289, s32[]{:T(128)} %get-tuple-element.288, bf16[10240,128]{1,0:T(8,128)(2,1)} %get-tuple-element.295, s32[512]{0:T(512)S(1)} %bitcast.77), kind=kOutput, calls=%fused_computation.10.clone.1.clone | convolution fusion | flops 1347485696 | bytes 2755072 | tf_op jit(solution)/shard_map/while/body/eval_jaxpr/dot_general | solution.py:68
  131.6 5.9 %fusion.52 = bf16[16,512,128]{2,1,0:T(8,128)(2,1)} fusion(bf16[16,512,128]{2,1,0:T(8,128)(2,1)} %get-tuple-element.289, s32[]{:T(128)} %get-tuple-element.288, bf16[10240,128]{1,0:T(8,128)(2,1)} %get-tuple-element.295, s32[512]{0:T(512)S(1)} %bitcast.77), kind=kOutput, calls=%fused_computation.10.clone.1.clone | convolution fusion | flops 1347485696 | bytes 2755072 | tf_op jit(solution)/shard_map/while/body/eval_jaxpr/dot_general | solution.py:68
  137.5 5.9 %fusion.52 = bf16[16,512,128]{2,1,0:T(8,128)(2,1)} fusion(bf16[16,512,128]{2,1,0:T(8,128)(2,1)} %get-tuple-element.289, s32[]{:T(128)} %get-tuple-element.288, bf16[10240,128]{1,0:T(8,128)(2,1)} %get-tuple-element.295, s32[512]{0:T(512)S(1)} %bitcast.77), kind=kOutput, calls=%fused_computation.10.clone.1.clone | convolution fusion | flops 1347485696 | bytes 2755072 | tf_op jit(solution)/shard_map/while/body/eval_jaxpr/dot_general | solution.py:68
  143.5 5.9 %fusion.52 = bf16[16,512,128]{2,1,0:T(8,128)(2,1)} fusion(bf16[16,512,128]{2,1,0:T(8,128)(2,1)} %get-tuple-element.289, s32[]{:T(128)} %get-tuple-element.288, bf16[10240,128]{1,0:T(8,128)(2,1)} %get-tuple-element.295, s32[512]{0:T(512)S(1)} %bitcast.77), kind=kOutput, calls=%fused_computation.10.clone.1.clone | convolution fusion | flops 1347485696 | bytes 2755072 | tf_op jit(solution)/shard_map/while/body/eval_jaxpr/dot_general | solution.py:68
  149.4 5.9 %fusion.52 = bf16[16,512,128]{2,1,0:T(8,128)(2,1)} fusion(bf16[16,512,128]{2,1,0:T(8,128)(2,1)} %get-tuple-element.289, s32[]{:T(128)} %get-tuple-element.288, bf16[10240,128]{1,0:T(8,128)(2,1)} %get-tuple-element.295, s32[512]{0:T(512)S(1)} %bitcast.77), kind=kOutput, calls=%fused_computation.10.clone.1.clone | convolution fusion | flops 1347485696 | bytes 2755072 | tf_op jit(solution)/shard_map/while/body/eval_jaxpr/dot_general | solution.py:68
  155.3 5.9 %fusion.52 = bf16[16,512,128]{2,1,0:T(8,128)(2,1)} fusion(bf16[16,512,128]{2,1,0:T(8,128)(2,1)} %get-tuple-element.289, s32[]{:T(128)} %get-tuple-element.288, bf16[10240,128]{1,0:T(8,128)(2,1)} %get-tuple-element.295, s32[512]{0:T(512)S(1)} %bitcast.77), kind=kOutput, calls=%fused_computation.10.clone.1.clone | convolution fusion | flops 1347485696 | bytes 2755072 | tf_op jit(solution)/shard_map/while/body/eval_jaxpr/dot_general | solution.py:68
  161.2 5.9 %fusion.52 = bf16[16,512,128]{2,1,0:T(8,128)(2,1)} fusion(bf16[16,512,128]{2,1,0:T(8,128)(2,1)} %get-tuple-element.289, s32[]{:T(128)} %get-tuple-element.288, bf16[10240,128]{1,0:T(8,128)(2,1)} %get-tuple-element.295, s32[512]{0:T(512)S(1)} %bitcast.77), kind=kOutput, calls=%fused_computation.10.clone.1.clone | convolution fusion | flops 1347485696 | bytes 2755072 | tf_op jit(solution)/shard_map/while/body/eval_jaxpr/dot_general | solution.py:68
  167.2 5.9 %fusion.52 = bf16[16,512,128]{2,1,0:T(8,128)(2,1)} fusion(bf16[16,512,128]{2,1,0:T(8,128)(2,1)} %get-tuple-element.289, s32[]{:T(128)} %get-tuple-element.288, bf16[10240,128]{1,0:T(8,128)(2,1)} %get-tuple-element.295, s32[512]{0:T(512)S(1)} %bitcast.77), kind=kOutput, calls=%fused_computation.10.clone.1.clone | convolution fusion | flops 1347485696 | bytes 2755072 | tf_op jit(solution)/shard_map/while/body/eval_jaxpr/dot_general | solution.py:68
  173.1 5.9 %fusion.52 = bf16[16,512,128]{2,1,0:T(8,128)(2,1)} fusion(bf16[16,512,128]{2,1,0:T(8,128)(2,1)} %get-tuple-element.289, s32[]{:T(128)} %get-tuple-element.288, bf16[10240,128]{1,0:T(8,128)(2,1)} %get-tuple-element.295, s32[512]{0:T(512)S(1)} %bitcast.77), kind=kOutput, calls=%fused_computation.10.clone.1.clone | convolution fusion | flops 1347485696 | bytes 2755072 | tf_op jit(solution)/shard_map/while/body/eval_jaxpr/dot_general | solution.py:68
  179.0 5.9 %fusion.52 = bf16[16,512,128]{2,1,0:T(8,128)(2,1)} fusion(bf16[16,512,128]{2,1,0:T(8,128)(2,1)} %get-tuple-element.289, s32[]{:T(128)} %get-tuple-element.288, bf16[10240,128]{1,0:T(8,128)(2,1)} %get-tuple-element.295, s32[512]{0:T(512)S(1)} %bitcast.77), kind=kOutput, calls=%fused_computation.10.clone.1.clone | convolution fusion | flops 1347485696 | bytes 2755072 | tf_op jit(solution)/shard_map/while/body/eval_jaxpr/dot_general | solution.py:68
  184.9 5.9 %fusion.52 = bf16[16,512,128]{2,1,0:T(8,128)(2,1)} fusion(bf16[16,512,128]{2,1,0:T(8,128)(2,1)} %get-tuple-element.289, s32[]{:T(128)} %get-tuple-element.288, bf16[10240,128]{1,0:T(8,128)(2,1)} %get-tuple-element.295, s32[512]{0:T(512)S(1)} %bitcast.77), kind=kOutput, calls=%fused_computation.10.clone.1.clone | convolution fusion | flops 1347485696 | bytes 2755072 | tf_op jit(solution)/shard_map/while/body/eval_jaxpr/dot_general | solution.py:68
  190.9 5.9 %fusion.52 = bf16[16,512,128]{2,1,0:T(8,128)(2,1)} fusion(bf16[16,512,128]{2,1,0:T(8,128)(2,1)} %get-tuple-element.289, s32[]{:T(128)} %get-tuple-element.288, bf16[10240,128]{1,0:T(8,128)(2,1)} %get-tuple-element.295, s32[512]{0:T(512)S(1)} %bitcast.77), kind=kOutput, calls=%fused_computation.10.clone.1.clone | convolution fusion | flops 1347485696 | bytes 2755072 | tf_op jit(solution)/shard_map/while/body/eval_jaxpr/dot_general | solution.py:68
  196.8 5.9 %fusion.52 = bf16[16,512,128]{2,1,0:T(8,128)(2,1)} fusion(bf16[16,512,128]{2,1,0:T(8,128)(2,1)} %get-tuple-element.289, s32[]{:T(128)} %get-tuple-element.288, bf16[10240,128]{1,0:T(8,128)(2,1)} %get-tuple-element.295, s32[512]{0:T(512)S(1)} %bitcast.77), kind=kOutput, calls=%fused_computation.10.clone.1.clone | convolution fusion | flops 1347485696 | bytes 2755072 | tf_op jit(solution)/shard_map/while/body/eval_jaxpr/dot_general | solution.py:68
  202.7 5.9 %fusion.52 = bf16[16,512,128]{2,1,0:T(8,128)(2,1)} fusion(bf16[16,512,128]{2,1,0:T(8,128)(2,1)} %get-tuple-element.289, s32[]{:T(128)} %get-tuple-element.288, bf16[10240,128]{1,0:T(8,128)(2,1)} %get-tuple-element.295, s32[512]{0:T(512)S(1)} %bitcast.77), kind=kOutput, calls=%fused_computation.10.clone.1.clone | convolution fusion | flops 1347485696 | bytes 2755072 | tf_op jit(solution)/shard_map/while/body/eval_jaxpr/dot_general | solution.py:68
  208.6 5.9 %fusion.52 = bf16[16,512,128]{2,1,0:T(8,128)(2,1)} fusion(bf16[16,512,128]{2,1,0:T(8,128)(2,1)} %get-tuple-element.289, s32[]{:T(128)} %get-tuple-element.288, bf16[10240,128]{1,0:T(8,128)(2,1)} %get-tuple-element.295, s32[512]{0:T(512)S(1)} %bitcast.77), kind=kOutput, calls=%fused_computation.10.clone.1.clone | convolution fusion | flops 1347485696 | bytes 2755072 | tf_op jit(solution)/shard_map/while/body/eval_jaxpr/dot_general | solution.py:68
  214.6 5.9 %fusion.52 = bf16[16,512,128]{2,1,0:T(8,128)(2,1)} fusion(bf16[16,512,128]{2,1,0:T(8,128)(2,1)} %get-tuple-element.289, s32[]{:T(128)} %get-tuple-element.288, bf16[10240,128]{1,0:T(8,128)(2,1)} %get-tuple-element.295, s32[512]{0:T(512)S(1)} %bitcast.77), kind=kOutput, calls=%fused_computation.10.clone.1.clone | convolution fusion | flops 1347485696 | bytes 2755072 | tf_op jit(solution)/shard_map/while/body/eval_jaxpr/dot_general | solution.py:68
  (149 shorter events, 7.5 us)
Async XLA Ops:
  0.0 41.8 %copy-start = (bf16[8192,128]{1,0:T(8,128)(2,1)S(1)}, bf16[8192,128]{1,0:T(8,128)(2,1)}, u32[]{:S(2)}) copy-start(bf16[8192,128]{1,0:T(8,128)(2,1)} %param.11) | copy-start | bytes 6291460
  84.4 41.3 %all-to-all-start.1 = ((bf16[128,80,128]{2,1,0:T(8,128)(2,1)}), bf16[128,80,128]{2,1,0:T(8,128)(2,1)}, u32[]{:S(2)}, u32[]{:S(2)}) async-start(bf16[128,80,128]{2,1,0:T(8,128)(2,1)} %broadcast_select_fusion.1), calls=%async_computation.1 | async-start | bytes 5242880 | tf_op jit(solution)/shard_map/all_to_all | solution.py:61
where the time goes:
time: 221 us; the launch traced here: 220 us
  matrix products  108 us (49%)
  local copies, waits for them, and re-layouts  38.1 us (17%)
  waiting for transfers between devices  36.4 us (16%)
  blocking collectives  21.2 us (10%)
  other arithmetic  10.9 us (5%)
  starting transfers between devices  4.83 us (2%)
    dot_general x16, matrix products, place_block(): jnp.dot(select, returned, preferred_element_type=jnp.float32)  94.7 us
    all_to_all x1, waiting for transfers between devices, on_device(): lax.all_to_all(replies, ('ep', 'dp'), split_axis=0, concat_axis=0, tiled=...  36.4 us
    gather x1, local copies, waits for them, and re-layouts, on_device(): replies = jnp.take(embedding_table, incoming, axis=0)  36.2 us
    all_to_all x1, blocking collectives, on_device(): lax.all_to_all(request, ('ep', 'dp'), split_axis=0, concat_axis=0, tiled=...  21.2 us
    dot_general x16, matrix products, rank_block(): lax.dot_general(weighted, rank_hot, (((0,), (0,)), ((), ())), precision=l...  8.31 us
    select_n x2, other arithmetic, on_device(): replies = jnp.take(embedding_table, incoming, axis=0)  6.47 us
    dot_general x16, matrix products, rank_block(): jnp.dot(earlier, hot.astype(jnp.bfloat16), preferred_element_type=jnp.flo...  5.02 us
    all_to_all x1, starting transfers between devices, on_device(): lax.all_to_all(replies, ('ep', 'dp'), split_axis=0, concat_axis=0, tiled=...  4.83 us
  transfers between devices with their start and end apart: 1, of which 1 were waited for; matrix products, arithmetic and copies ran while one was open for 0% of the time, Pallas kernels for 0%

commit v1 on v0

v1 whole, which is shorter than its diff:
```python
import functools

import jax
import jax.numpy as jnp
from jax import lax
from jax.experimental import pallas as pl
from jax.experimental.pallas import tpu as pltpu
from jax.sharding import PartitionSpec as P

LANES = 128
BLOCK = 256


def rank_kernel(per_owner, capacity, len_ref, slot_ref, ids_ref, req_ref, tgt_ref):
    feats, span = ids_ref.shape
    owners = req_ref.shape[0]
    owner_row = lax.broadcasted_iota(jnp.int32, (owners, BLOCK), 0)
    rank_row = lax.broadcasted_iota(jnp.int32, (capacity, BLOCK), 0).astype(jnp.float32)
    earlier = lax.broadcasted_iota(jnp.int32, (BLOCK, BLOCK + LANES), 0)
    later = lax.broadcasted_iota(jnp.int32, (BLOCK, BLOCK + LANES), 1)
    before_of = jnp.where(earlier < later, 1.0, 0.0).astype(jnp.bfloat16)
    lane = lax.broadcasted_iota(jnp.int32, (1, BLOCK), 1)
    offset = jnp.zeros((owners, LANES), jnp.float32)
    request = jnp.zeros((owners, capacity), jnp.float32)
    for f in range(feats):
        for at in range(0, span, BLOCK):
            ids = ids_ref[f : f + 1, at : at + BLOCK]
            valid = (lane + at) < len_ref[0, f]
            owner = ids // per_owner
            hot = owner_row == jnp.where(valid, owner, -1)
            hot_half = jnp.where(hot, 1.0, 0.0).astype(jnp.bfloat16)
            counted = jnp.dot(hot_half, before_of, preferred_element_type=jnp.float32)
            before = counted[:, :BLOCK] + jnp.concatenate([offset] * (BLOCK // LANES), axis=1)
            rank = jnp.sum(jnp.where(hot, before, 0.0), axis=0, keepdims=True)
            offset = offset + counted[:, BLOCK:]
            row = (ids - owner * per_owner) * feats + slot_ref[f]
            high = (row // 128).astype(jnp.float32)
            low = (row % 128).astype(jnp.float32)
            rank_hot = rank_row == rank
            ranked = jnp.concatenate(
                [
                    jnp.where(rank_hot, 128.0, 0.0).astype(jnp.bfloat16),
                    jnp.where(rank_hot, 1.0, 0.0).astype(jnp.bfloat16),
                ],
                axis=1,
            )
            weighted = jnp.concatenate(
                [
                    jnp.where(hot, high, 0.0).astype(jnp.bfloat16),
                    jnp.where(hot, low, 0.0).astype(jnp.bfloat16),
                ],
                axis=1,
            )
            request = request + lax.dot_general(
                weighted, ranked, (((1,), (1,)), ((), ())), preferred_element_type=jnp.float32
            )
            slot = owner * capacity + rank.astype(jnp.int32)
            tgt_ref[f : f + 1, at : at + BLOCK] = jnp.where(valid, slot, owners * capacity)
    req_ref[...] = request.astype(jnp.int32)


def widen(dst_ref, src_ref, step=256):
    def convert(i, _):
        at = pl.multiple_of(i * step, step)
        dst_ref[pl.ds(at, step), :] = src_ref[pl.ds(at, step), :].astype(jnp.float32)
        return 0

    lax.fori_loop(0, src_ref.shape[0] // step, convert, 0)


def lookup_kernel(inc_ref, tab_ref, out_ref, wide, stage):
    widen(wide, tab_ref)

    def body(d, _):
        for r in range(out_ref.shape[1]):
            stage[r : r + 1, :] = wide[pl.ds(inc_ref[d, r], 1), :]
        out_ref[d] = stage[...].astype(out_ref.dtype)
        return 0

    lax.fori_loop(0, out_ref.shape[0], body, 0)


def place_kernel(tgt_ref, ret_ref, out_ref, wide, stage):
    slots = ret_ref.shape[0]
    span = out_ref.shape[1]
    group = stage.shape[0]
    widen(wide, ret_ref)
    wide[slots:, :] = jnp.zeros((wide.shape[0] - slots, wide.shape[1]), jnp.float32)

    def body(k, _):
        f = k // (span // group)
        at = pl.multiple_of((k % (span // group)) * group, group)
        for r in range(group):
            stage[r : r + 1, :] = wide[pl.ds(tgt_ref[f, at + r], 1), :]
        out_ref[f, pl.ds(at, group), :] = stage[...].astype(out_ref.dtype)
        return 0

    lax.fori_loop(0, out_ref.shape[0] * (span // group), body, 0)


def on_device(lengths, id_lists, feature_slots, embedding_table):
    num_users, num_feats, list_span = id_lists.shape
    row_width = embedding_table.shape[1]
    owners = lax.axis_size("ep") * lax.axis_size("dp")
    per_owner = embedding_table.shape[0] // num_feats
    slot_total = num_users * num_feats * list_span
    capacity = 5 * slot_total // (4 * owners)
    axes = ("ep", "dp")
    smem = pl.BlockSpec(memory_space=pltpu.SMEM)
    vmem = pl.BlockSpec(memory_space=pltpu.VMEM)

    request, targets = pl.pallas_call(
        functools.partial(rank_kernel, per_owner, capacity),
        out_shape=(
            jax.ShapeDtypeStruct((owners, capacity), jnp.int32),
            jax.ShapeDtypeStruct((num_feats, list_span), jnp.int32),
        ),
        in_specs=[smem, smem, vmem],
        out_specs=(vmem, vmem),
        name="rank_ids",
    )(lengths, feature_slots, id_lists.reshape(num_feats, list_span))
    incoming = lax.all_to_all(request, axes, split_axis=0, concat_axis=0, tiled=True)
    replies = pl.pallas_call(
        lookup_kernel,
        out_shape=jax.ShapeDtypeStruct((owners, capacity, row_width), embedding_table.dtype),
        in_specs=[smem, vmem],
        out_specs=vmem,
        scratch_shapes=[
            pltpu.VMEM(embedding_table.shape, jnp.float32),
            pltpu.VMEM((capacity, row_width), jnp.float32),
        ],
        name="lookup_rows",
    )(incoming, embedding_table)
    returned = lax.all_to_all(replies, axes, split_axis=0, concat_axis=0, tiled=True)
    returned = returned.reshape(owners * capacity, row_width)
    embedded = pl.pallas_call(
        place_kernel,
        out_shape=jax.ShapeDtypeStruct((num_feats, list_span, row_width), embedding_table.dtype),
        in_specs=[smem, vmem],
        out_specs=vmem,
        scratch_shapes=[
            pltpu.VMEM((owners * capacity + 8, row_width), jnp.float32),
            pltpu.VMEM((64, row_width), jnp.float32),
        ],
        name="place_rows",
    )(targets, returned)
    return embedded.reshape(num_users, num_feats, list_span, row_width)


def solution(mesh):
    placed = (P(("ep", "dp"), None), P(("ep", "dp"), None, None), P(), P(("ep", "dp"), None))
    return jax.shard_map(
        on_device,
        mesh=mesh,
        in_specs=placed,
        out_specs=P(("ep", "dp"), None, None, None),
        check_vma=False,
    )
```

time: 221 us -> 107 us (0.48)
  matrix products: 108 us -> 0 us
  Pallas kernels: 0 us -> 43.3 us
  blocking collectives: 21.2 us -> 63.2 us
  local copies, waits for them, and re-layouts: 38.1 us -> 0 us
  waiting for transfers between devices: 36.4 us -> 0 us
  other arithmetic: 10.9 us -> 0 us
  starting transfers between devices: 4.83 us -> 0 us
    dot_general x48 -> x0, matrix products: 108 us -> none  [the longest x16 94.7 us: place_block(): jnp.dot(select, returned, preferred_element_type=jnp.float32)]
    pallas_call x0 -> x3, Pallas kernels: none -> 43.3 us  [the longest x1 24.9 us: on_device(): pl.pallas_call(place_kernel, out_shape=jax.ShapeDtypeStruct((num_feats, l...]
    all_to_all x1 -> x2, blocking collectives: 21.2 us -> 63.2 us  [the longest x1 41.3 us: on_device(): lax.all_to_all(replies, axes, split_axis=0, concat_axis=0, tiled=True)]
    all_to_all x1 -> x0, waiting for transfers between devices: 36.4 us -> none  [on_device(): lax.all_to_all(replies, ('ep', 'dp'), split_axis=0, concat_axis=0, tiled=...]
    gather x1 -> x0, local copies, waits for them, and re-layouts: 36.2 us -> none  [on_device(): replies = jnp.take(embedding_table, incoming, axis=0)]
    select_n x18 -> x0, other arithmetic: 6.79 us -> none  [the longest x2 6.47 us: on_device(): replies = jnp.take(embedding_table, incoming, axis=0)]
    all_to_all x1 -> x0, starting transfers between devices: 4.83 us -> none  [on_device(): lax.all_to_all(replies, ('ep', 'dp'), split_axis=0, concat_axis=0, tiled=...]
  transfers between devices with their start and end apart: 1 -> 0, of which waited for: 1 -> 0; matrix products, arithmetic and copies ran while one was open for 0% -> 0% of each run, Pallas kernels for 0% -> 0%
where the time goes in v1:
time: 107 us; the launch traced here: 106 us
  blocking collectives  63.2 us (59%)
  Pallas kernels  43.3 us (40%)
    all_to_all x1, blocking collectives, on_device(): lax.all_to_all(replies, axes, split_axis=0, concat_axis=0, tiled=True)  41.3 us
    pallas_call x1, Pallas kernels, on_device(): pl.pallas_call(place_kernel, out_shape=jax.ShapeDtypeStruct((num_feats, l...  24.9 us
    all_to_all x1, blocking collectives, on_device(): lax.all_to_all(request, axes, split_axis=0, concat_axis=0, tiled=True)  21.9 us
    pallas_call x1, Pallas kernels, on_device(): pl.pallas_call(lookup_kernel, out_shape=jax.ShapeDtypeStruct((owners, cap...  14.2 us
    pallas_call x1, Pallas kernels, on_device(): pl.pallas_call(functools.partial(rank_kernel, per_owner, capacity), out_s...  4.2 us

profile of v1, /device:TPU:1, one launch (start us, length us, event | category | flops | bytes accessed | tf_op | source)
XLA Modules:
  0.0 106.5 jit_solution(9860188370777440574)
XLA Ops:
  0.0 4.2 %rank_ids.1 = (s32[128,80]{1,0:T(8,128)}, s32[16,512]{1,0:T(8,128)}) custom-call(s32[1,16]{1,0:T(1,128)} %len_ref.1, s32[16]{0:T(128)} %slot_ref.1, s32[16,512]{1,0:T(8,128)} %bitcast.10), custom_call_target="tpu_custom_call" | custom-call | tf_op jit(solution)/shard_map/rank_ids/pallas_call | solution.py:112
  4.2 21.9 %all_to_all.16 = s32[128,1,80]{2,1,0:T(1,128)} all-to-all(s32[128,1,80]{2,1,0:T(1,128)} %bitcast.9), channel_id=1, replica_groups=mesh['ep'=32,'dp'=4] {'ep','dp'}, dimensions={0} | all-to-all | bytes 81920 | tf_op jit(solution)/shard_map/all_to_all | solution.py:122
  26.1 14.2 %lookup_rows.1 = bf16[128,80,128]{2,1,0:T(8,128)(2,1)} custom-call(s32[128,80]{1,0:T(8,128)} %bitcast.8, bf16[8192,128]{1,0:T(8,128)(2,1)} %tab_ref.1), custom_call_target="tpu_custom_call" | custom-call | tf_op jit(solution)/shard_map/lookup_rows/pallas_call | solution.py:123
  40.3 41.3 %all_to_all.17 = bf16[128,80,128]{2,1,0:T(8,128)(2,1)} all-to-all(bf16[128,80,128]{2,1,0:T(8,128)(2,1)} %lookup_rows.1), channel_id=1, replica_groups=mesh['ep'=32,'dp'=4] {'ep','dp'}, dimensions={0} | all-to-all | bytes 5242880 | tf_op jit(solution)/shard_map/all_to_all | solution.py:134
  81.6 24.9 %place_rows.1 = bf16[16,512,128]{2,1,0:T(8,128)(2,1)} custom-call(s32[16,512]{1,0:T(8,128)} %get-tuple-element.7.tgt_ref, bf16[10240,128]{1,0:T(8,128)(2,1)} %bitcast.7), custom_call_target="tpu_custom_call" | custom-call | tf_op jit(solution)/shard_map/place_rows/pallas_call | solution.py:136

commit v2 on v1

v2 whole, which is shorter than its diff:
```python
import functools

import jax
import jax.numpy as jnp
from jax import lax
from jax.experimental import pallas as pl
from jax.experimental.pallas import tpu as pltpu
from jax.sharding import PartitionSpec as P

LANES = 128
BLOCK = 256
GROUP = 16
WINDOW = 64
MIB = 2**20


def rank_kernel(
    per_owner,
    capacity,
    len_hbm,
    slot_hbm,
    ids_hbm,
    tab_hbm,
    req_ref,
    tgt_ref,
    wide_ref,
    len_ref,
    slot_ref,
    ids_ref,
    tab_ref,
    sems,
):
    copies = [
        pltpu.make_async_copy(src, dst, sems.at[k])
        for k, (src, dst) in enumerate(
            [(len_hbm, len_ref), (slot_hbm, slot_ref), (ids_hbm, ids_ref), (tab_hbm, tab_ref)]
        )
    ]
    for copy in copies:
        copy.start()
    feats, span = ids_ref.shape
    owners = req_ref.shape[0]
    owner_row = lax.broadcasted_iota(jnp.int32, (owners, BLOCK), 0)
    rank_row = lax.broadcasted_iota(jnp.int32, (capacity, BLOCK), 0).astype(jnp.float32)
    earlier = lax.broadcasted_iota(jnp.int32, (BLOCK, BLOCK + LANES), 0)
    later = lax.broadcasted_iota(jnp.int32, (BLOCK, BLOCK + LANES), 1)
    before_of = jnp.where(earlier < later, 1.0, 0.0).astype(jnp.bfloat16)
    lane = lax.broadcasted_iota(jnp.int32, (1, BLOCK), 1)
    offset = jnp.zeros((owners, LANES), jnp.float32)
    request = jnp.zeros((owners, capacity), jnp.float32)
    for copy in copies[:3]:
        copy.wait()
    steps = feats * (span // BLOCK)
    for step in range(steps):
        f, at = step // (span // BLOCK), step % (span // BLOCK) * BLOCK
        ids = ids_ref[f : f + 1, at : at + BLOCK]
        valid = (lane + at) < len_ref[0, f]
        owner = ids // per_owner
        hot = owner_row == jnp.where(valid, owner, -1)
        hot_half = jnp.where(hot, 1.0, 0.0).astype(jnp.bfloat16)
        counted = jnp.dot(hot_half, before_of, preferred_element_type=jnp.float32)
        before = counted[:, :BLOCK] + jnp.concatenate([offset] * (BLOCK // LANES), axis=1)
        rank = jnp.sum(jnp.where(hot, before, 0.0), axis=0, keepdims=True)
        offset = offset + counted[:, BLOCK:]
        row = (ids - owner * per_owner) * feats + slot_ref[f]
        high = (row // 128).astype(jnp.float32)
        low = (row % 128).astype(jnp.float32)
        rank_hot = rank_row == rank
        ranked = jnp.concatenate(
            [
                jnp.where(rank_hot, 128.0, 0.0).astype(jnp.bfloat16),
                jnp.where(rank_hot, 1.0, 0.0).astype(jnp.bfloat16),
            ],
            axis=1,
        )
        weighted = jnp.concatenate(
            [
                jnp.where(hot, high, 0.0).astype(jnp.bfloat16),
                jnp.where(hot, low, 0.0).astype(jnp.bfloat16),
            ],
            axis=1,
        )
        request = request + lax.dot_general(
            weighted, ranked, (((1,), (1,)), ((), ())), preferred_element_type=jnp.float32
        )
        slot = owner * capacity + rank.astype(jnp.int32)
        slot = jnp.where(valid, slot, owners * capacity)
        for part in range(BLOCK // LANES):
            line = f * (span // LANES) + at // LANES + part
            tgt_ref[line : line + 1, :] = slot[:, part * LANES : (part + 1) * LANES]
    copies[3].wait()
    widen(wide_ref, tab_ref)
    req_ref[:, :capacity] = request.astype(jnp.int32)
    req_ref[:, capacity:] = offset[:, capacity:].astype(jnp.int32)


def widen(dst_ref, src_ref, step=256):
    def convert(i, _):
        at = pl.multiple_of(i * step, step)
        dst_ref[pl.ds(at, step), :] = src_ref[pl.ds(at, step), :].astype(jnp.float32)
        return 0

    lax.fori_loop(0, src_ref.shape[0] // step, convert, 0)


def lookup_kernel(capacity, inc_ref, wide_ref, out_ref, stage):
    def body(d, _):
        count = inc_ref[d, capacity]
        for g in range(0, capacity, GROUP):

            @pl.when(count > g)
            def _():
                for r in range(g, g + GROUP):
                    stage[r : r + 1, :] = wide_ref[pl.ds(inc_ref[d, r], 1), :]

        out_ref[d] = stage[...].astype(out_ref.dtype)
        return 0

    lax.fori_loop(0, out_ref.shape[0], body, 0)


def place_kernel(len_ref, tgt_ref, ret_ref, out_hbm, wide, stage, out_ref, sem):
    slots = ret_ref.shape[0]
    feats, span = out_ref.shape[:2]
    widen(wide, ret_ref)
    wide[slots:, :] = jnp.zeros((wide.shape[0] - slots, wide.shape[1]), jnp.float32)
    zeros = jnp.zeros((WINDOW, wide.shape[1]), out_ref.dtype)

    def feature(f, _):
        used = (len_ref[0, f] + (WINDOW - 1)) // WINDOW

        def filled(k, _):
            for h in range(LANES // WINDOW):

                @pl.when(k % (LANES // WINDOW) == h)
                def _():
                    line = f * (span // LANES) + k // (LANES // WINDOW)
                    for r in range(WINDOW):
                        stage[r : r + 1, :] = wide[pl.ds(tgt_ref[line, h * WINDOW + r], 1), :]

            out_ref[f, pl.ds(pl.multiple_of(k * WINDOW, WINDOW), WINDOW), :] = stage[...].astype(out_ref.dtype)
            return 0

        def blank(k, _):
            out_ref[f, pl.ds(pl.multiple_of(k * WINDOW, WINDOW), WINDOW), :] = zeros
            return 0

        lax.fori_loop(0, used, filled, 0)
        lax.fori_loop(used, span // WINDOW, blank, 0)
        pltpu.make_async_copy(out_ref.at[f], out_hbm.at[f], sem).start()
        return 0

    lax.fori_loop(0, feats, feature, 0)
    pltpu.make_async_copy(out_ref, out_hbm, sem).wait()


def on_device(lengths, id_lists, feature_slots, embedding_table):
    num_users, num_feats, list_span = id_lists.shape
    rows, row_width = embedding_table.shape
    owners = lax.axis_size("ep") * lax.axis_size("dp")
    per_owner = rows // num_feats
    slot_total = num_users * num_feats * list_span
    capacity = 5 * slot_total // (4 * owners)
    axes = ("ep", "dp")
    dtype = embedding_table.dtype
    smem = pl.BlockSpec(memory_space=pltpu.SMEM)
    vmem = pl.BlockSpec(memory_space=pltpu.VMEM)
    hbm = pl.BlockSpec(memory_space=pltpu.HBM)
    ids = id_lists.reshape(num_feats, list_span)

    request, targets, wide = pl.pallas_call(
        functools.partial(rank_kernel, per_owner, capacity),
        out_shape=(
            pltpu.VMEM((owners, LANES), jnp.int32),
            pltpu.VMEM((slot_total // LANES, LANES), jnp.int32),
            pltpu.VMEM((rows, row_width), jnp.float32),
        ),
        in_specs=[hbm] * 4,
        out_specs=(vmem,) * 3,
        scratch_shapes=[
            pltpu.SMEM(lengths.shape, jnp.int32),
            pltpu.SMEM(feature_slots.shape, jnp.int32),
            pltpu.VMEM(ids.shape, jnp.int32),
            pltpu.VMEM((rows, row_width), dtype),
            pltpu.SemaphoreType.DMA((4,)),
        ],
        compiler_params=pltpu.CompilerParams(vmem_limit_bytes=16 * MIB),
        name="rank_ids",
    )(*(pltpu.with_memory_space_constraint(x, pltpu.HBM) for x in (lengths, feature_slots, ids, embedding_table)))
    incoming = lax.all_to_all(request, axes, split_axis=0, concat_axis=0, tiled=True)
    replies = pl.pallas_call(
        functools.partial(lookup_kernel, capacity),
        out_shape=jax.ShapeDtypeStruct((owners, capacity, row_width), dtype),
        in_specs=[smem, vmem],
        out_specs=vmem,
        scratch_shapes=[pltpu.VMEM((capacity, row_width), jnp.float32)],
        compiler_params=pltpu.CompilerParams(vmem_limit_bytes=16 * MIB),
        name="lookup_rows",
    )(incoming, wide)
    returned = lax.all_to_all(replies, axes, split_axis=0, concat_axis=0, tiled=True)
    returned = returned.reshape(owners * capacity, row_width)
    embedded = pl.pallas_call(
        place_kernel,
        out_shape=jax.ShapeDtypeStruct((num_feats, list_span, row_width), dtype),
        in_specs=[smem, smem, vmem],
        out_specs=hbm,
        scratch_shapes=[
            pltpu.VMEM((owners * capacity + 8, row_width), jnp.float32),
            pltpu.VMEM((WINDOW, row_width), jnp.float32),
            pltpu.VMEM((num_feats, list_span, row_width), dtype),
            pltpu.SemaphoreType.DMA,
        ],
        compiler_params=pltpu.CompilerParams(vmem_limit_bytes=20 * MIB),
        name="place_rows",
    )(pltpu.with_memory_space_constraint(lengths, pltpu.HBM), targets, returned)
    return embedded.reshape(num_users, num_feats, list_span, row_width)


def solution(mesh):
    placed = (P(("ep", "dp"), None), P(("ep", "dp"), None, None), P(), P(("ep", "dp"), None))
    return jax.shard_map(
        on_device,
        mesh=mesh,
        in_specs=placed,
        out_specs=P(("ep", "dp"), None, None, None),
        check_vma=False,
    )
```

time: 107 us -> 88.4 us (0.83)
  Pallas kernels: 43.3 us -> 23.7 us
  blocking collectives: 63.2 us -> 64.8 us
    pallas_call x1, Pallas kernels: 24.9 us -> 9.86 us  [on_device(): pl.pallas_call(place_kernel, out_shape=jax.ShapeDtypeStruct((num_feats, l...]
    pallas_call x1, Pallas kernels: 14.2 us -> 9.99 us  [on_device(): pl.pallas_call(functools.partial(lookup_kernel, capacity), out_shape=jax....]
    all_to_all x1, blocking collectives: 41.3 us -> 43.6 us  [on_device(): lax.all_to_all(replies, axes, split_axis=0, concat_axis=0, tiled=True)]
where the time goes in v2:
time: 88.4 us; the launch traced here: 88.6 us
  blocking collectives  64.8 us (73%)
  Pallas kernels  23.7 us (27%)
    all_to_all x1, blocking collectives, on_device(): lax.all_to_all(replies, axes, split_axis=0, concat_axis=0, tiled=True)  43.6 us
    all_to_all x1, blocking collectives, on_device(): lax.all_to_all(request, axes, split_axis=0, concat_axis=0, tiled=True)  21.2 us
    pallas_call x1, Pallas kernels, on_device(): pl.pallas_call(functools.partial(lookup_kernel, capacity), out_shape=jax....  9.99 us
    pallas_call x1, Pallas kernels, on_device(): pl.pallas_call(place_kernel, out_shape=jax.ShapeDtypeStruct((num_feats, l...  9.86 us
    pallas_call x1, Pallas kernels, on_device(): pl.pallas_call(functools.partial(rank_kernel, per_owner, capacity), out_s...  3.88 us

profile of v2, /device:TPU:1, one launch (start us, length us, event | category | flops | bytes accessed | tf_op | source)
XLA Modules:
  0.0 88.6 jit_solution(6211510282530894626)
XLA Ops:
  0.0 3.9 %rank_ids.1 = (s32[128,128]{1,0:T(8,128)S(1)}, s32[64,128]{1,0:T(8,128)S(1)}, f32[8192,128]{1,0:T(8,128)S(1)}) custom-call(s32[1,16]{1,0:T(1,128)} %len_ref.1, s32[16]{0:T(128)} %slot_hbm.1, s32[16,512]{1,0:T(8,128)} %bitcast.10, bf16[8192,128]{1,0:T(8,128)(2,1)} %tab_hbm.1), custom_call_target="tpu_custom_call" | custom-call | tf_op jit(solution)/shard_map/rank_ids/pallas_call | solution.py:171
  3.9 21.2 %all_to_all.16 = s32[128,1,128]{2,1,0:T(1,128)S(1)} all-to-all(s32[128,1,128]{2,1,0:T(1,128)S(1)} %bitcast.9), channel_id=1, replica_groups=mesh['ep'=32,'dp'=4] {'ep','dp'}, dimensions={0} | all-to-all | bytes 131072 | tf_op jit(solution)/shard_map/all_to_all | solution.py:190
  25.1 10.0 %lookup_rows.1 = bf16[128,80,128]{2,1,0:T(8,128)(2,1)S(1)} custom-call(s32[128,128]{1,0:T(8,128)S(1)} %bitcast.8, f32[8192,128]{1,0:T(8,128)S(1)} %get-tuple-element.10.wide_ref), custom_call_target="tpu_custom_call" | custom-call | tf_op jit(solution)/shard_map/lookup_rows/pallas_call | solution.py:191
  35.1 43.6 %all_to_all.17 = bf16[128,80,128]{2,1,0:T(8,128)(2,1)S(1)} all-to-all(bf16[128,80,128]{2,1,0:T(8,128)(2,1)S(1)} %lookup_rows.1), channel_id=1, replica_groups=mesh['ep'=32,'dp'=4] {'ep','dp'}, dimensions={0} | all-to-all | bytes 5242880 | tf_op jit(solution)/shard_map/all_to_all | solution.py:200
  78.7 9.9 %place_rows.1 = bf16[16,512,128]{2,1,0:T(8,128)(2,1)} custom-call(s32[1,16]{1,0:T(1,128)} %len_ref.1, s32[64,128]{1,0:T(8,128)S(1)} %get-tuple-element.8.tgt_ref, bf16[10240,128]{1,0:T(8,128)(2,1)S(1)} %bitcast.7), custom_call_target="tpu_custom_call" | custom-call | tf_op jit(solution)/shard_map/place_rows/pallas_call | solution.py:202

commit v3 on v2

--- a/solution.py
+++ b/solution.py
@@ -11,6 +11,8 @@
 BLOCK = 256
 GROUP = 16
 WINDOW = 64
+PAD = 8
+DEPTH = 4
 MIB = 2**20
 
 
@@ -91,67 +93,100 @@
     copies[3].wait()
     widen(wide_ref, tab_ref)
     req_ref[:, :capacity] = request.astype(jnp.int32)
-    req_ref[:, capacity:] = offset[:, capacity:].astype(jnp.int32)
+    req_ref[:, capacity:] = jnp.zeros((owners, LANES - capacity), jnp.int32)
 
 
 def widen(dst_ref, src_ref, step=256):
     def convert(i, _):
         at = pl.multiple_of(i * step, step)
-        dst_ref[pl.ds(at, step), :] = src_ref[pl.ds(at, step), :].astype(jnp.float32)
+        dst_ref[pl.ds(at + PAD, step), :] = src_ref[pl.ds(at, step), :].astype(jnp.float32)
         return 0
 
     lax.fori_loop(0, src_ref.shape[0] // step, convert, 0)
 
 
-def lookup_kernel(capacity, inc_ref, wide_ref, out_ref, stage):
-    def body(d, _):
-        count = inc_ref[d, capacity]
-        for g in range(0, capacity, GROUP):
-
-            @pl.when(count > g)
+def gather_rows(wide_ref, index_of, count):
+    sublane = lax.broadcasted_iota(jnp.int32, (8, wide_ref.shape[1]), 0)
+    tiles = []
+    for base in range(0, count, 8):
+        tile = wide_ref[pl.ds(index_of(base) + PAD, 8), :]
+        for r in range(1, 8):
+            tile = jnp.where(sublane == r, wide_ref[pl.ds(index_of(base + r) + (PAD - r), 8), :], tile)
+        tiles.append(tile)
+    return jnp.concatenate(tiles, axis=0)
+
+
+def in_windows(source_ref, buffers, sems, body):
+    lines = buffers[0].shape[0]
+    windows = source_ref.shape[0] // lines
+    depth = len(buffers)
+
+    def fetch(w, b):
+        at = pl.multiple_of(w * lines, lines)
+        return pltpu.make_async_copy(source_ref.at[pl.ds(at, lines)], buffers[b], sems.at[b])
+
+    for b in range(depth):
+        fetch(b, b).start()
+
+    def turn(k, _):
+        for b in range(depth):
+            w = k * depth + b
+            fetch(w, b).wait()
+            body(w, buffers[b])
+
+            @pl.when(w + depth < windows)
             def _():
-                for r in range(g, g + GROUP):
-                    stage[r : r + 1, :] = wide_ref[pl.ds(inc_ref[d, r], 1), :]
-
-        out_ref[d] = stage[...].astype(out_ref.dtype)
+                fetch(w + depth, b).start()
+
         return 0
 
-    lax.fori_loop(0, out_ref.shape[0], body, 0)
-
-
-def place_kernel(len_ref, tgt_ref, ret_ref, out_hbm, wide, stage, out_ref, sem):
+    return lambda: lax.fori_loop(0, windows // depth, turn, 0)
+
+
+def lookup_kernel(inc_ref, wide_ref, out_ref, sems, *buffers):
+    capacity = out_ref.shape[1]
+
+    def window(w, index_ref):
+        lines = index_ref.shape[0]
+        for d in range(lines):
+            for g in range(0, capacity, GROUP):
+                rows = gather_rows(wide_ref, lambda r: index_ref[d, g + r], GROUP)
+                out_ref[w * lines + d, g : g + GROUP, :] = rows.astype(out_ref.dtype)
+
+    in_windows(inc_ref, buffers, sems, window)()
+
+
+def place_kernel(len_hbm, tgt_ref, ret_ref, out_hbm, len_ref, wide, out_ref, out_sem, len_sem, sems, *buffers):
     slots = ret_ref.shape[0]
     feats, span = out_ref.shape[:2]
+    zeros = jnp.zeros((WINDOW, wide.shape[1]), out_ref.dtype)
+    lengths_copy = pltpu.make_async_copy(len_hbm, len_ref, len_sem)
+    lengths_copy.start()
+
+    def feature(f, index_ref):
+        used = len_ref[0, f]
+        for at in range(0, span, WINDOW):
+
+            @pl.when(used > at)
+            def _():
+                for g in range(at, at + WINDOW, GROUP):
+                    rows = gather_rows(
+                        wide, lambda r: index_ref[(g + r) // LANES, (g + r) % LANES], GROUP
+                    )
+                    out_ref[f, g : g + GROUP, :] = rows.astype(out_ref.dtype)
+
+            @pl.when(used <= at)
+            def _():
+                out_ref[f, at : at + WINDOW, :] = zeros
+
+        pltpu.make_async_copy(out_ref.at[f], out_hbm.at[f], out_sem).start()
+
+    run = in_windows(tgt_ref, buffers, sems, feature)
     widen(wide, ret_ref)
-    wide[slots:, :] = jnp.zeros((wide.shape[0] - slots, wide.shape[1]), jnp.float32)
-    zeros = jnp.zeros((WINDOW, wide.shape[1]), out_ref.dtype)
-
-    def feature(f, _):
-        used = (len_ref[0, f] + (WINDOW - 1)) // WINDOW
-
-        def filled(k, _):
-            for h in range(LANES // WINDOW):
-
-                @pl.when(k % (LANES // WINDOW) == h)
-                def _():
-                    line = f * (span // LANES) + k // (LANES // WINDOW)
-                    for r in range(WINDOW):
-                        stage[r : r + 1, :] = wide[pl.ds(tgt_ref[line, h * WINDOW + r], 1), :]
-
-            out_ref[f, pl.ds(pl.multiple_of(k * WINDOW, WINDOW), WINDOW), :] = stage[...].astype(out_ref.dtype)
-            return 0
-
-        def blank(k, _):
-            out_ref[f, pl.ds(pl.multiple_of(k * WINDOW, WINDOW), WINDOW), :] = zeros
-            return 0
-
-        lax.fori_loop(0, used, filled, 0)
-        lax.fori_loop(used, span // WINDOW, blank, 0)
-        pltpu.make_async_copy(out_ref.at[f], out_hbm.at[f], sem).start()
-        return 0
-
-    lax.fori_loop(0, feats, feature, 0)
-    pltpu.make_async_copy(out_ref, out_hbm, sem).wait()
+    wide[PAD + slots :, :] = jnp.zeros((wide.shape[0] - slots - PAD, wide.shape[1]), jnp.float32)
+    lengths_copy.wait()
+    run()
+    pltpu.make_async_copy(out_ref, out_hbm, out_sem).wait()
 
 
 def on_device(lengths, id_lists, feature_slots, embedding_table):
@@ -163,7 +198,6 @@
     capacity = 5 * slot_total // (4 * owners)
     axes = ("ep", "dp")
     dtype = embedding_table.dtype
-    smem = pl.BlockSpec(memory_space=pltpu.SMEM)
     vmem = pl.BlockSpec(memory_space=pltpu.VMEM)
     hbm = pl.BlockSpec(memory_space=pltpu.HBM)
     ids = id_lists.reshape(num_feats, list_span)
@@ -173,7 +207,7 @@
         out_shape=(
             pltpu.VMEM((owners, LANES), jnp.int32),
             pltpu.VMEM((slot_total // LANES, LANES), jnp.int32),
-            pltpu.VMEM((rows, row_width), jnp.float32),
+            pltpu.VMEM((PAD + rows + PAD, row_width), jnp.float32),
         ),
         in_specs=[hbm] * 4,
         out_specs=(vmem,) * 3,
@@ -189,11 +223,11 @@
     )(*(pltpu.with_memory_space_constraint(x, pltpu.HBM) for x in (lengths, feature_slots, ids, embedding_table)))
     incoming = lax.all_to_all(request, axes, split_axis=0, concat_axis=0, tiled=True)
     replies = pl.pallas_call(
-        functools.partial(lookup_kernel, capacity),
+        lookup_kernel,
         out_shape=jax.ShapeDtypeStruct((owners, capacity, row_width), dtype),
-        in_specs=[smem, vmem],
+        in_specs=[vmem, vmem],
         out_specs=vmem,
-        scratch_shapes=[pltpu.VMEM((capacity, row_width), jnp.float32)],
+        scratch_shapes=[pltpu.SemaphoreType.DMA((DEPTH,))] + [pltpu.SMEM((8, LANES), jnp.int32)] * DEPTH,
         compiler_params=pltpu.CompilerParams(vmem_limit_bytes=16 * MIB),
         name="lookup_rows",
     )(incoming, wide)
@@ -202,14 +236,17 @@
     embedded = pl.pallas_call(
         place_kernel,
         out_shape=jax.ShapeDtypeStruct((num_feats, list_span, row_width), dtype),
-        in_specs=[smem, smem, vmem],
+        in_specs=[hbm, vmem, vmem],
         out_specs=hbm,
         scratch_shapes=[
-            pltpu.VMEM((owners * capacity + 8, row_width), jnp.float32),
-            pltpu.VMEM((WINDOW, row_width), jnp.float32),
+            pltpu.SMEM(lengths.shape, jnp.int32),
+            pltpu.VMEM((PAD + owners * capacity + 2 * PAD, row_width), jnp.float32),
             pltpu.VMEM((num_feats, list_span, row_width), dtype),
             pltpu.SemaphoreType.DMA,
-        ],
+            pltpu.SemaphoreType.DMA,
+            pltpu.SemaphoreType.DMA((DEPTH,)),
+        ]
+        + [pltpu.SMEM((list_span // LANES, LANES), jnp.int32)] * DEPTH,
         compiler_params=pltpu.CompilerParams(vmem_limit_bytes=20 * MIB),
         name="place_rows",
     )(pltpu.with_memory_space_constraint(lengths, pltpu.HBM), targets, returned)

time: 88.4 us -> 77.7 us (0.88)
  Pallas kernels: 23.7 us -> 15.8 us
  blocking collectives: 64.8 us -> 61.7 us
    pallas_call x1, Pallas kernels: 9.86 us -> 5.6 us  [on_device(): pl.pallas_call(place_kernel, out_shape=jax.ShapeDtypeStruct((num_feats, l...]
    pallas_call x1, Pallas kernels: 9.99 us -> 6.25 us  [on_device(): pl.pallas_call(lookup_kernel, out_shape=jax.ShapeDtypeStruct((owners, cap...]
    all_to_all x1, blocking collectives: 43.6 us -> 40.4 us  [on_device(): lax.all_to_all(replies, axes, split_axis=0, concat_axis=0, tiled=True)]
where the time goes in v3:
time: 77.7 us; the launch traced here: 77.5 us
  blocking collectives  61.7 us (79%)
  Pallas kernels  15.8 us (20%)
    all_to_all x1, blocking collectives, on_device(): lax.all_to_all(replies, axes, split_axis=0, concat_axis=0, tiled=True)  40.4 us
    all_to_all x1, blocking collectives, on_device(): lax.all_to_all(request, axes, split_axis=0, concat_axis=0, tiled=True)  21.2 us
    pallas_call x1, Pallas kernels, on_device(): pl.pallas_call(lookup_kernel, out_shape=jax.ShapeDtypeStruct((owners, cap...  6.25 us
    pallas_call x1, Pallas kernels, on_device(): pl.pallas_call(place_kernel, out_shape=jax.ShapeDtypeStruct((num_feats, l...  5.6 us
    pallas_call x1, Pallas kernels, on_device(): pl.pallas_call(functools.partial(rank_kernel, per_owner, capacity), out_s...  3.95 us

profile of v3, /device:TPU:1, one launch (start us, length us, event | category | flops | bytes accessed | tf_op | source)
XLA Modules:
  0.0 77.5 jit_solution(3768183428642978373)
XLA Ops:
  0.0 4.0 %rank_ids.1 = (s32[128,128]{1,0:T(8,128)S(1)}, s32[64,128]{1,0:T(8,128)S(1)}, f32[8208,128]{1,0:T(8,128)S(1)}) custom-call(s32[1,16]{1,0:T(1,128)} %len_hbm.3, s32[16]{0:T(128)} %slot_hbm.1, s32[16,512]{1,0:T(8,128)} %bitcast.10, bf16[8192,128]{1,0:T(8,128)(2,1)} %tab_hbm.1), custom_call_target="tpu_custom_call" | custom-call | tf_op jit(solution)/shard_map/rank_ids/pallas_call | solution.py:205
  4.0 21.2 %all_to_all.16 = s32[128,1,128]{2,1,0:T(1,128)S(1)} all-to-all(s32[128,1,128]{2,1,0:T(1,128)S(1)} %bitcast.9), channel_id=1, replica_groups=mesh['ep'=32,'dp'=4] {'ep','dp'}, dimensions={0} | all-to-all | bytes 131072 | tf_op jit(solution)/shard_map/all_to_all | solution.py:224
  25.2 6.2 %lookup_rows.1 = bf16[128,80,128]{2,1,0:T(8,128)(2,1)S(1)} custom-call(s32[128,128]{1,0:T(8,128)S(1)} %bitcast.8, f32[8208,128]{1,0:T(8,128)S(1)} %get-tuple-element.10.wide_ref), custom_call_target="tpu_custom_call" | custom-call | tf_op jit(solution)/shard_map/lookup_rows/pallas_call | solution.py:225
  31.4 40.4 %all_to_all.17 = bf16[128,80,128]{2,1,0:T(8,128)(2,1)S(1)} all-to-all(bf16[128,80,128]{2,1,0:T(8,128)(2,1)S(1)} %lookup_rows.1), channel_id=1, replica_groups=mesh['ep'=32,'dp'=4] {'ep','dp'}, dimensions={0} | all-to-all | bytes 5242880 | tf_op jit(solution)/shard_map/all_to_all | solution.py:234
  71.9 5.6 %place_rows.1 = bf16[16,512,128]{2,1,0:T(8,128)(2,1)} custom-call(s32[1,16]{1,0:T(1,128)} %len_hbm.3, s32[64,128]{1,0:T(8,128)S(1)} %get-tuple-element.8.tgt_ref, bf16[10240,128]{1,0:T(8,128)(2,1)S(1)} %bitcast.7), custom_call_target="tpu_custom_call" | custom-call | tf_op jit(solution)/shard_map/place_rows/pallas_call | solution.py:236

commit v4 on v3

--- a/solution.py
+++ b/solution.py
@@ -10,9 +10,10 @@
 LANES = 128
 BLOCK = 256
 GROUP = 16
-WINDOW = 64
+WINDOW = 256
 PAD = 8
 DEPTH = 4
+CHAIN = 8
 MIB = 2**20
 
 
@@ -25,11 +26,10 @@
     tab_hbm,
     req_ref,
     tgt_ref,
-    wide_ref,
+    tab_ref,
     len_ref,
     slot_ref,
     ids_ref,
-    tab_ref,
     sems,
 ):
     copies = [
@@ -42,58 +42,81 @@
         copy.start()
     feats, span = ids_ref.shape
     owners = req_ref.shape[0]
-    owner_row = lax.broadcasted_iota(jnp.int32, (owners, BLOCK), 0)
-    rank_row = lax.broadcasted_iota(jnp.int32, (capacity, BLOCK), 0).astype(jnp.float32)
-    earlier = lax.broadcasted_iota(jnp.int32, (BLOCK, BLOCK + LANES), 0)
-    later = lax.broadcasted_iota(jnp.int32, (BLOCK, BLOCK + LANES), 1)
-    before_of = jnp.where(earlier < later, 1.0, 0.0).astype(jnp.bfloat16)
-    lane = lax.broadcasted_iota(jnp.int32, (1, BLOCK), 1)
-    offset = jnp.zeros((owners, LANES), jnp.float32)
-    request = jnp.zeros((owners, capacity), jnp.float32)
+    half = jnp.bfloat16
+    one, zero = jnp.ones((16, BLOCK), half), jnp.zeros((16, BLOCK), half)
+    row_of = lax.broadcasted_iota(jnp.int32, (16, BLOCK), 0).astype(jnp.float32)
+    owner_rows = [(row_of + 16 * t).astype(half) for t in range(owners // 16)]
+    rank_rows = [(row_of + (16 * t + 1)).astype(half) for t in range(capacity // 16)]
+    earlier = lax.broadcasted_iota(jnp.int32, (BLOCK, BLOCK), 0)
+    later = lax.broadcasted_iota(jnp.int32, (BLOCK, BLOCK), 1)
+    up_to = jnp.where(earlier <= later, 1.0, 0.0).astype(half)
+    feature = lax.broadcasted_iota(jnp.int32, (feats, LANES), 0)
+    lane = lax.broadcasted_iota(jnp.int32, (feats, span), 1)
     for copy in copies[:3]:
         copy.wait()
-    steps = feats * (span // BLOCK)
-    for step in range(steps):
-        f, at = step // (span // BLOCK), step % (span // BLOCK) * BLOCK
-        ids = ids_ref[f : f + 1, at : at + BLOCK]
-        valid = (lane + at) < len_ref[0, f]
-        owner = ids // per_owner
-        hot = owner_row == jnp.where(valid, owner, -1)
-        hot_half = jnp.where(hot, 1.0, 0.0).astype(jnp.bfloat16)
-        counted = jnp.dot(hot_half, before_of, preferred_element_type=jnp.float32)
-        before = counted[:, :BLOCK] + jnp.concatenate([offset] * (BLOCK // LANES), axis=1)
-        rank = jnp.sum(jnp.where(hot, before, 0.0), axis=0, keepdims=True)
-        offset = offset + counted[:, BLOCK:]
-        row = (ids - owner * per_owner) * feats + slot_ref[f]
-        high = (row // 128).astype(jnp.float32)
-        low = (row % 128).astype(jnp.float32)
-        rank_hot = rank_row == rank
-        ranked = jnp.concatenate(
-            [
-                jnp.where(rank_hot, 128.0, 0.0).astype(jnp.bfloat16),
-                jnp.where(rank_hot, 1.0, 0.0).astype(jnp.bfloat16),
-            ],
-            axis=1,
+    length = jnp.zeros((feats, LANES), jnp.int32)
+    slot = jnp.zeros((feats, LANES), jnp.int32)
+    for f in range(feats):
+        length = jnp.where(feature == f, len_ref[0, f], length)
+        slot = jnp.where(feature == f, slot_ref[f], slot)
+    ids = ids_ref[...]
+    valid = lane < jnp.concatenate([length] * (span // LANES), axis=1)
+    owner = ids >> (per_owner.bit_length() - 1)
+    row = (ids & (per_owner - 1)) * feats + jnp.concatenate([slot] * (span // LANES), axis=1)
+    base = jnp.where(valid, owner * capacity - 1, owners * capacity).astype(jnp.float32)
+    owner = jnp.where(valid, owner, -1).astype(jnp.float32)
+    high, low = (row >> 7).astype(jnp.float32), (row & 127).astype(jnp.float32)
+
+    offset = [jnp.zeros((16, LANES), half) for _ in owner_rows]
+    request = jnp.zeros((owners, 2 * capacity), jnp.float32)
+    per_feature = span // BLOCK
+    for first in range(0, feats * per_feature, CHAIN):
+        hots, wanted = [], []
+        for step in range(first, first + CHAIN):
+            f, at = step // per_feature, step % per_feature * BLOCK
+
+            def spread(x):
+                return jnp.broadcast_to(x, (16, BLOCK)).astype(half)
+
+            def line(x):
+                return x[f : f + 1, at : at + BLOCK]
+
+            key = spread(line(owner))
+            hot = [jnp.where(rows == key, one, zero) for rows in owner_rows]
+            hots.append(jnp.concatenate(hot, axis=0))
+            counted = jnp.dot(hots[-1], up_to, preferred_element_type=jnp.float32)
+            total = jnp.broadcast_to(counted[:, BLOCK - 1 :], (owners, LANES)).astype(half)
+            counted = counted.astype(half)
+            picked = zero
+            for t in range(len(hot)):
+                at_t = slice(16 * t, 16 * t + 16)
+                before = counted[at_t] + jnp.concatenate([offset[t]] * (BLOCK // LANES), axis=1)
+                picked = picked + hot[t] * before
+                offset[t] = offset[t] + total[at_t]
+            rank = jnp.sum(picked.astype(jnp.float32), axis=0, keepdims=True)
+            key, high_of, low_of = spread(rank), spread(line(high)), spread(line(low))
+            found = [rows == key for rows in rank_rows]
+            wanted.append(
+                jnp.concatenate(
+                    [jnp.where(x, high_of, zero) for x in found]
+                    + [jnp.where(x, low_of, zero) for x in found],
+                    axis=0,
+                )
+            )
+            place = (line(base) + rank).astype(jnp.int32)
+            for part in range(BLOCK // LANES):
+                at_line = f * (span // LANES) + at // LANES + part
+                tgt_ref[at_line : at_line + 1, :] = place[:, part * LANES : (part + 1) * LANES]
+        request = request + lax.dot_general(
+            jnp.concatenate(hots, axis=1),
+            jnp.concatenate(wanted, axis=1),
+            (((1,), (1,)), ((), ())),
+            preferred_element_type=jnp.float32,
         )
-        weighted = jnp.concatenate(
-            [
-                jnp.where(hot, high, 0.0).astype(jnp.bfloat16),
-                jnp.where(hot, low, 0.0).astype(jnp.bfloat16),
-            ],
-            axis=1,
-        )
-        request = request + lax.dot_general(
-            weighted, ranked, (((1,), (1,)), ((), ())), preferred_element_type=jnp.float32
-        )
-        slot = owner * capacity + rank.astype(jnp.int32)
-        slot = jnp.where(valid, slot, owners * capacity)
-        for part in range(BLOCK // LANES):
-            line = f * (span // LANES) + at // LANES + part
-            tgt_ref[line : line + 1, :] = slot[:, part * LANES : (part + 1) * LANES]
+    asked = request[:, :capacity] * 128.0 + request[:, capacity:]
+    req_ref[:, :capacity] = asked.astype(jnp.int32)
+    req_ref[:, capacity:] = jnp.zeros((owners, LANES - capacity), jnp.int32)
     copies[3].wait()
-    widen(wide_ref, tab_ref)
-    req_ref[:, :capacity] = request.astype(jnp.int32)
-    req_ref[:, capacity:] = jnp.zeros((owners, LANES - capacity), jnp.int32)
 
 
 def widen(dst_ref, src_ref, step=256):
@@ -143,7 +166,7 @@
     return lambda: lax.fori_loop(0, windows // depth, turn, 0)
 
 
-def lookup_kernel(inc_ref, wide_ref, out_ref, sems, *buffers):
+def lookup_kernel(inc_ref, tab_ref, out_ref, wide_ref, sems, *buffers):
     capacity = out_ref.shape[1]
 
     def window(w, index_ref):
@@ -153,7 +176,9 @@
                 rows = gather_rows(wide_ref, lambda r: index_ref[d, g + r], GROUP)
                 out_ref[w * lines + d, g : g + GROUP, :] = rows.astype(out_ref.dtype)
 
-    in_windows(inc_ref, buffers, sems, window)()
+    run = in_windows(inc_ref, buffers, sems, window)
+    widen(wide_ref, tab_ref)
+    run()
 
 
 def place_kernel(len_hbm, tgt_ref, ret_ref, out_hbm, len_ref, wide, out_ref, out_sem, len_sem, sems, *buffers):
@@ -202,12 +227,12 @@
     hbm = pl.BlockSpec(memory_space=pltpu.HBM)
     ids = id_lists.reshape(num_feats, list_span)
 
-    request, targets, wide = pl.pallas_call(
+    request, targets, table = pl.pallas_call(
         functools.partial(rank_kernel, per_owner, capacity),
         out_shape=(
             pltpu.VMEM((owners, LANES), jnp.int32),
             pltpu.VMEM((slot_total // LANES, LANES), jnp.int32),
-            pltpu.VMEM((PAD + rows + PAD, row_width), jnp.float32),
+            pltpu.VMEM((rows, row_width), dtype),
         ),
         in_specs=[hbm] * 4,
         out_specs=(vmem,) * 3,
@@ -215,7 +240,6 @@
             pltpu.SMEM(lengths.shape, jnp.int32),
             pltpu.SMEM(feature_slots.shape, jnp.int32),
             pltpu.VMEM(ids.shape, jnp.int32),
-            pltpu.VMEM((rows, row_width), dtype),
             pltpu.SemaphoreType.DMA((4,)),
         ],
         compiler_params=pltpu.CompilerParams(vmem_limit_bytes=16 * MIB),
@@ -227,10 +251,14 @@
         out_shape=jax.ShapeDtypeStruct((owners, capacity, row_width), dtype),
         in_specs=[vmem, vmem],
         out_specs=vmem,
-        scratch_shapes=[pltpu.SemaphoreType.DMA((DEPTH,))] + [pltpu.SMEM((8, LANES), jnp.int32)] * DEPTH,
+        scratch_shapes=[
+            pltpu.VMEM((PAD + rows + PAD, row_width), jnp.float32),
+            pltpu.SemaphoreType.DMA((DEPTH,)),
+        ]
+        + [pltpu.SMEM((8, LANES), jnp.int32)] * DEPTH,
         compiler_params=pltpu.CompilerParams(vmem_limit_bytes=16 * MIB),
         name="lookup_rows",
-    )(incoming, wide)
+    )(incoming, table)
     returned = lax.all_to_all(replies, axes, split_axis=0, concat_axis=0, tiled=True)
     returned = returned.reshape(owners * capacity, row_width)
     embedded = pl.pallas_call(

time: 77.7 us -> 76.4 us (0.983)
  Pallas kernels: 15.8 us -> 14.3 us
    pallas_call x1, Pallas kernels: 3.95 us -> 2.79 us  [on_device(): pl.pallas_call(functools.partial(rank_kernel, per_owner, capacity), out_s...]
where the time goes in v4:
time: 76.4 us; the launch traced here: 76 us
  blocking collectives  61.7 us (81%)
  Pallas kernels  14.3 us (19%)
    all_to_all x1, blocking collectives, on_device(): lax.all_to_all(replies, axes, split_axis=0, concat_axis=0, tiled=True)  40.4 us
    all_to_all x1, blocking collectives, on_device(): lax.all_to_all(request, axes, split_axis=0, concat_axis=0, tiled=True)  21.2 us
    pallas_call x1, Pallas kernels, on_device(): pl.pallas_call(lookup_kernel, out_shape=jax.ShapeDtypeStruct((owners, cap...  6.25 us
    pallas_call x1, Pallas kernels, on_device(): pl.pallas_call(place_kernel, out_shape=jax.ShapeDtypeStruct((num_feats, l...  5.25 us
    pallas_call x1, Pallas kernels, on_device(): pl.pallas_call(functools.partial(rank_kernel, per_owner, capacity), out_s...  2.79 us

profile of v4, /device:TPU:1, one launch (start us, length us, event | category | flops | bytes accessed | tf_op | source)
XLA Modules:
  0.0 76.0 jit_solution(7595346717630841655)
XLA Ops:
  0.0 2.8 %rank_ids.1 = (s32[128,128]{1,0:T(8,128)S(1)}, s32[64,128]{1,0:T(8,128)S(1)}, bf16[8192,128]{1,0:T(8,128)(2,1)S(1)}) custom-call(s32[1,16]{1,0:T(1,128)} %len_hbm.3, s32[16]{0:T(128)} %slot_hbm.1, s32[16,512]{1,0:T(8,128)} %bitcast.10, bf16[8192,128]{1,0:T(8,128)(2,1)} %tab_hbm.1), custom_call_target="tpu_custom_call" | custom-call | tf_op jit(solution)/shard_map/rank_ids/pallas_call | solution.py:230
  2.8 21.2 %all_to_all.16 = s32[128,1,128]{2,1,0:T(1,128)S(1)} all-to-all(s32[128,1,128]{2,1,0:T(1,128)S(1)} %bitcast.9), channel_id=1, replica_groups=mesh['ep'=32,'dp'=4] {'ep','dp'}, dimensions={0} | all-to-all | bytes 131072 | tf_op jit(solution)/shard_map/all_to_all | solution.py:248
  24.0 6.3 %lookup_rows.1 = bf16[128,80,128]{2,1,0:T(8,128)(2,1)S(1)} custom-call(s32[128,128]{1,0:T(8,128)S(1)} %bitcast.8, bf16[8192,128]{1,0:T(8,128)(2,1)S(1)} %get-tuple-element.10.tab_ref), custom_call_target="tpu_custom_call" | custom-call | tf_op jit(solution)/shard_map/lookup_rows/pallas_call | solution.py:249
  30.3 40.4 %all_to_all.17 = bf16[128,80,128]{2,1,0:T(8,128)(2,1)S(1)} all-to-all(bf16[128,80,128]{2,1,0:T(8,128)(2,1)S(1)} %lookup_rows.1), channel_id=1, replica_groups=mesh['ep'=32,'dp'=4] {'ep','dp'}, dimensions={0} | all-to-all | bytes 5242880 | tf_op jit(solution)/shard_map/all_to_all | solution.py:262
  70.7 5.2 %place_rows.1 = bf16[16,512,128]{2,1,0:T(8,128)(2,1)} custom-call(s32[1,16]{1,0:T(1,128)} %len_hbm.3, s32[64,128]{1,0:T(8,128)S(1)} %get-tuple-element.8.tgt_ref, bf16[10240,128]{1,0:T(8,128)(2,1)S(1)} %bitcast.7), custom_call_target="tpu_custom_call" | custom-call | tf_op jit(solution)/shard_map/place_rows/pallas_call | solution.py:264
